TPU v7x, 128 devices: a whole 4x4x4 slice. The times are simulated.
128 devices in a mesh: expert: 4 (over x_lo, core), shard: 32 (over z, y, x_hi).
Axes of the slice: x: 4 (x_hi: 2, x_lo: 2; x = x_hi * 2 + x_lo), y: 4, z: 4, core: 2. Of those that a mesh axis runs over, the one named last changes fastest.
Arguments:
- master_gate: float32 [64, 2048, 1024], P('expert', 'shard'), may hold values from -0.25 to 0.25
- master_up: float32 [64, 2048, 1024], P('expert', 'shard'), may hold values from -0.25 to 0.25
- master_down: float32 [64, 1024, 2048], P('expert', None, 'shard'), may hold values from -0.375 to 0.375
- router_weight: float32 [2048, 64], P('shard', 'expert'), may hold values from -0.125 to 0.125
- router_gain: float32 [2048], P('shard'), may hold values from 0.25 to 1.75
Outputs:
- final_gate: bfloat16 [64, 2048, 1024], P('expert', None, 'shard')
- final_up: bfloat16 [64, 2048, 1024], P('expert', None, 'shard')
- final_down: bfloat16 [64, 1024, 2048], P('expert', 'shard')
- scale_gate: float32 [64, 1024], P('expert', 'shard')
- scale_up: float32 [64, 1024], P('expert', 'shard')
- scale_down: float32 [64, 1024], P('expert', 'shard')
- serve_router: bfloat16 [2048, 64], replicated
All inputs are finite; a program needn't handle non-finite values.
Results may differ from a plain program's by a relative error of at most 0.001.
Values may be sent and summed in bfloat16 or wider, within the bound.
A program may use at most 128 MiB of HBM per device.

v0:
```python
import jax
import jax.numpy as jnp
from jax import lax
from jax.sharding import Mesh
from jax.sharding import PartitionSpec as P

SHARD = ("shard_0", "shard_1", "shard_2")
EXPERT = ("expert_0", "expert_1")


def total_of_pieces(value, axis):
    return lax.all_gather(value, axis).sum(0)


def in_order(pieces, dim):
    pieces = jnp.moveaxis(pieces, 0, dim)
    lengths = pieces.shape
    return pieces.reshape(*lengths[:dim], lengths[dim] * lengths[dim + 1], *lengths[dim + 2 :])


def gather_in_order(value, axes, order):
    pieces = value[None]
    for k in order:
        pieces = lax.all_gather(pieces, axes[k], axis=0, tiled=True)
    current = [lax.axis_size(axes[k]) for k in reversed(order)]
    pieces = pieces.reshape(*current, *value.shape)
    turned = sorted(range(len(order)), key=lambda place: order[len(order) - 1 - place])
    return pieces.transpose(*turned, *range(len(order), pieces.ndim)).reshape(-1, *value.shape)


def whole_of(value, axes, order, dim):
    return in_order(gather_in_order(value, axes, order), dim)


def on_device(master_gate, master_up, master_down, router_weight, router_gain):
    total_gate, total_up, total_down = (
        total_of_pieces(jnp.sum(master_gate * master_gate, axis=1), SHARD),
        total_of_pieces(jnp.sum(master_up * master_up, axis=1), SHARD),
        total_of_pieces(jnp.sum(master_down * master_down, axis=2), SHARD),
    )
    scale_gate = jnp.sqrt(total_gate)
    scale_up = jnp.sqrt(total_up)
    scale_down = jnp.sqrt(total_down)
    narrow_gate, narrow_up, narrow_down = (
        (master_gate / jnp.expand_dims(scale_gate, 1)).astype(jnp.bfloat16),
        (master_up / jnp.expand_dims(scale_up, 1)).astype(jnp.bfloat16),
        (master_down / jnp.expand_dims(scale_down, 2)).astype(jnp.bfloat16),
    )
    final_gate, final_up = (
        lax.all_to_all(narrow_gate, SHARD, split_axis=2, concat_axis=1, tiled=True),
        lax.all_to_all(narrow_up, SHARD, split_axis=2, concat_axis=1, tiled=True),
    )
    final_down = lax.all_to_all(narrow_down, SHARD, split_axis=1, concat_axis=2, tiled=True)
    scale_gate = lax.dynamic_slice_in_dim(
        scale_gate, lax.axis_index(SHARD) * final_gate.shape[2], final_gate.shape[2], axis=1
    )
    scale_up = lax.dynamic_slice_in_dim(
        scale_up, lax.axis_index(SHARD) * final_up.shape[2], final_up.shape[2], axis=1
    )
    scale_down = lax.dynamic_slice_in_dim(
        scale_down, lax.axis_index(SHARD) * final_down.shape[1], final_down.shape[1], axis=1
    )
    part_router = (router_weight * router_gain[:, None]).astype(jnp.bfloat16)
    row_router = whole_of(part_router, SHARD, (2, 0, 1), 0)
    serve_router = whole_of(row_router, EXPERT, (0, 1), 1)
    return (final_gate, final_up, final_down, scale_gate, scale_up, scale_down, serve_router)


def solution(mesh):
    torus = Mesh(
        mesh.devices.reshape(2, 2, 4, 4, 2),
        ("expert_0", "expert_1", "shard_0", "shard_1", "shard_2"),
    )
    return jax.shard_map(
        on_device,
        mesh=torus,
        in_specs=(
            P(EXPERT, SHARD, None),
            P(EXPERT, SHARD, None),
            P(EXPERT, None, SHARD),
            P(SHARD, EXPERT),
            P(SHARD),
        ),
        out_specs=(
            P(EXPERT, None, SHARD),
            P(EXPERT, None, SHARD),
            P(EXPERT, SHARD, None),
            P(EXPERT, SHARD),
            P(EXPERT, SHARD),
            P(EXPERT, SHARD),
            P(),
        ),
        check_vma=False,
    )
```

profile of v0, /device:TPU:0, one launch (start us, length us, event | category | flops | bytes accessed | tf_op | source)
XLA Modules:
  0.0 397.6 jit_solution(14546526943388077372)
XLA Ops:
  7.2 3.4 multiply_reduce_fusion.2
  10.7 3.4 multiply_reduce_fusion.1
  14.2 3.4 multiply_reduce_fusion
  17.6 8.1 %copy.42 = f32[16,64,1024]{1,0,2:T(8,128)} copy(f32[16,64,1024]{2,1,0:T(8,128)} %param.5) | data formatting | bytes 8388608 | tf_op args[0]
  25.8 58.9 %all-gather.9.cloned.1.call-done = f32[512,1024]{1,0:T(8,128)} async-done(((f32[16,1024]{1,0:T(8,128)}), f32[512,1024]{1,0:T(8,128)}) %all-gather.9.cloned.1.call-update) | async-done | bytes 2097168 | tf_op jit(solution)/shard_map/all_gather | solution.py:12
  86.6 6.9 %fusion.1 = bf16[1024,16,64]{2,1,0:T(8,128)(2,1)} fusion(f32[16,64,1024]{1,0,2:T(8,128)} %copy.42, f32[16,1024]{0,1:T(8,128)S(1)} %copy.41), kind=kLoop, calls=%fused_computation.12 | loop fusion | flops 2097152 | bytes 6356992
  93.5 7.9 %reshape.47 = bf16[32,2,16384]{2,1,0:T(2,128)(2,1)} reshape(bf16[1024,16,64]{2,1,0:T(8,128)(2,1)} %fusion.1) | data formatting | bytes 4194304
  101.3 5.8 %all-to-all-start = ((bf16[32,2,16384]{2,1,0:T(2,128)(2,1)}), bf16[32,2,16384]{2,1,0:T(2,128)(2,1)S(1)}, u32[]{:S(2)}, u32[]{:S(2)}) async-start(bf16[32,2,16384]{2,1,0:T(2,128)(2,1)} %reshape.47), calls=%async_computation | async-start | bytes 4194304 | tf_op jit(solution)/shard_map/all_to_all | solution.py:50
  107.2 8.1 %copy.46 = f32[16,64,1024]{1,0,2:T(8,128)} copy(f32[16,64,1024]{2,1,0:T(8,128)} %param.6) | data formatting | bytes 8388608 | tf_op args[1]
  115.3 51.8 %all-gather.11.cloned.1.call-done = f32[512,1024]{1,0:T(8,128)} async-done(((f32[16,1024]{1,0:T(8,128)}), f32[512,1024]{1,0:T(8,128)}) %all-gather.11.cloned.1.call-update) | async-done | bytes 2097168 | tf_op jit(solution)/shard_map/all_gather | solution.py:12
  169.0 6.9 %fusion.2 = bf16[1024,16,64]{2,1,0:T(8,128)(2,1)} fusion(f32[16,64,1024]{1,0,2:T(8,128)} %copy.46, f32[16,1024]{0,1:T(8,128)S(1)} %copy.45), kind=kLoop, calls=%fused_computation.13 | loop fusion | flops 2097152 | bytes 6356992
  175.9 7.9 %reshape.49 = bf16[32,2,16384]{2,1,0:T(2,128)(2,1)} reshape(bf16[1024,16,64]{2,1,0:T(8,128)(2,1)} %fusion.2) | data formatting | bytes 4194304
  183.8 6.0 %all-to-all-start.1 = ((bf16[32,2,16384]{2,1,0:T(2,128)(2,1)}), bf16[32,2,16384]{2,1,0:T(2,128)(2,1)}, u32[]{:S(2)}, u32[]{:S(2)}) async-start(bf16[32,2,16384]{2,1,0:T(2,128)(2,1)} %reshape.49), calls=%async_computation.1 | async-start | bytes 4194304 | tf_op jit(solution)/shard_map/all_to_all | solution.py:51
  189.8 8.1 %copy.50 = f32[16,1024,64]{2,0,1:T(8,128)} copy(f32[16,1024,64]{1,2,0:T(8,128)} %param.7) | data formatting | bytes 8388608 | tf_op args[2]
  197.9 51.7 %all-gather.13.cloned.1.call-done = f32[512,1024]{1,0:T(8,128)} async-done(((f32[16,1024]{1,0:T(8,128)}), f32[512,1024]{1,0:T(8,128)}) %all-gather.13.cloned.1.call-update) | async-done | bytes 2097168 | tf_op jit(solution)/shard_map/all_gather | solution.py:12
  251.5 6.9 %fusion.3 = bf16[1024,16,64]{2,1,0:T(8,128)(2,1)} fusion(f32[16,1024,64]{2,0,1:T(8,128)} %copy.50, f32[16,1024]{0,1:T(8,128)S(1)} %copy.49), kind=kLoop, calls=%fused_computation.14 | loop fusion | flops 2097152 | bytes 6356992
  258.4 7.9 %reshape.51 = bf16[32,2,16384]{2,1,0:T(2,128)(2,1)} reshape(bf16[1024,16,64]{2,1,0:T(8,128)(2,1)} %fusion.3) | data formatting | bytes 4194304
  266.3 6.0 %all-to-all-start.2 = ((bf16[32,2,16384]{2,1,0:T(2,128)(2,1)}), bf16[32,2,16384]{2,1,0:T(2,128)(2,1)}, u32[]{:S(2)}, u32[]{:S(2)}) async-start(bf16[32,2,16384]{2,1,0:T(2,128)(2,1)} %reshape.51), calls=%async_computation.2 | async-start | bytes 4194304 | tf_op jit(solution)/shard_map/all_to_all | solution.py:53
  272.3 24.1 %all-gather.4 = bf16[2,64,16]{1,2,0:T(8,128)(2,1)S(1)} all-gather(bf16[1,64,16]{1,2,0:T(8,128)(2,1)S(1)} %fusion), channel_id=5, replica_groups=mesh['expert_0'=2,'expert_1'=2,'shard_0'=4,'shard_1'=4,'shard_2'=2] {'sh..., dimensions={0}, use_global_device_ids=true | all-gather | bytes 6144 | tf_op jit(solution)/shard_map/all_gather | solution.py:24
  296.4 12.2 %all_gather.40 = bf16[8,64,16]{1,2,0:T(8,128)(2,1)S(1)} all-gather(bf16[2,64,16]{1,2,0:T(8,128)(2,1)S(1)} %all-gather.4), channel_id=1, replica_groups=mesh['expert_0'=2,'expert_1'=2,'shard_0'=4,'shard_1'=4,'shard_2'=2] {'sh..., dimensions={0}, use_global_device_ids=true | all-gather | bytes 20480 | tf_op jit(solution)/shard_map/all_gather | solution.py:24
  308.6 12.5 %all_gather.41 = bf16[32,64,16]{1,2,0:T(8,128)(2,1)S(1)} all-gather(bf16[8,64,16]{1,2,0:T(8,128)(2,1)S(1)} %all_gather.40), channel_id=1, replica_groups=mesh['expert_0'=2,'expert_1'=2,'shard_0'=4,'shard_1'=4,'shard_2'=2] {'sh..., dimensions={0}, use_global_device_ids=true | all-gather | bytes 81920 | tf_op jit(solution)/shard_map/all_gather | solution.py:24
  321.4 4.9 %all_gather.42 = bf16[2,2048,16]{1,2,0:T(8,128)(2,1)S(1)} all-gather(bf16[1,2048,16]{1,2,0:T(8,128)(2,1)S(1)} %broadcast_in_dim_reshape_reshape.3), channel_id=1, replica_groups=mesh['expert_0'=2,'expert_1'=2,'shard_0'=4,'shard_1'=4,'shard_2'=2] {'ex..., dimensions={0}, use_global_device_ids=true | all-gather | bytes 196608 | tf_op jit(solution)/shard_map/all_gather | solution.py:24
  326.3 2.0 all_gather.43
  330.4 4.0 %reshape.48 = bf16[1024,16,64]{2,1,0:T(8,128)(2,1)} reshape(bf16[32,2,16384]{2,1,0:T(2,128)(2,1)S(1)} %all-to-all-done) | data formatting | bytes 4194304
  334.4 6.9 %copy.44 = bf16[16,32,64,32]{2,1,3,0:T(8,128)(2,1)} copy(bf16[16,32,64,32]{2,0,3,1:T(8,128)(2,1)} %bitcast.47) | data formatting | bytes 4194304 | tf_op jit(solution)/shard_map/all_to_all | solution.py:50
  341.2 6.7 %all_to_all.42 = bf16[16,2048,32]{1,2,0:T(8,128)(2,1)} reshape(bf16[16,32,64,32]{2,1,3,0:T(8,128)(2,1)} %copy.44) | data formatting | bytes 4194304 | tf_op jit(solution)/shard_map/all_to_all | solution.py:50
  348.0 7.9 %reshape.50 = bf16[1024,16,64]{2,1,0:T(8,128)(2,1)} reshape(bf16[32,2,16384]{2,1,0:T(2,128)(2,1)} %all-to-all-done.1) | data formatting | bytes 4194304
  355.9 6.9 %copy.48 = bf16[16,32,64,32]{2,1,3,0:T(8,128)(2,1)} copy(bf16[16,32,64,32]{2,0,3,1:T(8,128)(2,1)} %bitcast.48) | data formatting | bytes 4194304 | tf_op jit(solution)/shard_map/all_to_all | solution.py:51
  362.8 6.7 %all_to_all.46 = bf16[16,2048,32]{1,2,0:T(8,128)(2,1)} reshape(bf16[16,32,64,32]{2,1,3,0:T(8,128)(2,1)} %copy.48) | data formatting | bytes 4194304 | tf_op jit(solution)/shard_map/all_to_all | solution.py:51
  369.5 7.9 %reshape.52 = bf16[1024,16,64]{2,1,0:T(8,128)(2,1)} reshape(bf16[32,2,16384]{2,1,0:T(2,128)(2,1)} %all-to-all-done.2) | data formatting | bytes 4194304
  377.4 6.9 %copy.52 = bf16[16,32,32,64]{3,2,1,0:T(8,128)(2,1)} copy(bf16[16,32,32,64]{3,0,1,2:T(8,128)(2,1)} %bitcast.49) | data formatting | bytes 4194304 | tf_op jit(solution)/shard_map/all_to_all | solution.py:53
  384.3 6.7 %all_to_all.50 = bf16[16,32,2048]{2,1,0:T(8,128)(2,1)} reshape(bf16[16,32,32,64]{3,2,1,0:T(8,128)(2,1)} %copy.52) | data formatting | bytes 4194304 | tf_op jit(solution)/shard_map/all_to_all | solution.py:53
  (28 shorter events, 8.3 us)
Async XLA Ops:
  7.2 77.5 %all-gather.9.cloned.1.call-start = ((), (), s32[]{:S(2)}) async-start(), calls=%async_computation.3 | async-start | bytes 2162688 | tf_op jit(solution)/shard_map/all_gather | solution.py:12
  10.7 156.4 %all-gather.11.cloned.1.call-start = ((), (), s32[]{:S(2)}) async-start(), calls=%async_computation.4 | async-start | bytes 2162688 | tf_op jit(solution)/shard_map/all_gather | solution.py:12
  14.1 235.4 %all-gather.13.cloned.1.call-start = ((), (), s32[]{:S(2)}) async-start(), calls=%async_computation.5 | async-start | bytes 2162688 | tf_op jit(solution)/shard_map/all_gather | solution.py:12
  101.3 82.4 %all-to-all-start = ((bf16[32,2,16384]{2,1,0:T(2,128)(2,1)}), bf16[32,2,16384]{2,1,0:T(2,128)(2,1)S(1)}, u32[]{:S(2)}, u32[]{:S(2)}) async-start(bf16[32,2,16384]{2,1,0:T(2,128)(2,1)} %reshape.47), calls=%async_computation | async-start | bytes 4194304 | tf_op jit(solution)/shard_map/all_to_all | solution.py:50
  183.8 82.5 %all-to-all-start.1 = ((bf16[32,2,16384]{2,1,0:T(2,128)(2,1)}), bf16[32,2,16384]{2,1,0:T(2,128)(2,1)}, u32[]{:S(2)}, u32[]{:S(2)}) async-start(bf16[32,2,16384]{2,1,0:T(2,128)(2,1)} %reshape.49), calls=%async_computation.1 | async-start | bytes 4194304 | tf_op jit(solution)/shard_map/all_to_all | solution.py:51
  258.4 13.9 %copy-start = (f32[64,16]{0,1:T(8,128)S(1)}, f32[64,16]{0,1:T(8,128)}, u32[]{:S(2)}) copy-start(f32[64,16]{0,1:T(8,128)} %param.8) | copy-start | bytes 12292
  258.4 13.9 %copy-start.1 = (f32[64]{0:T(128)S(1)}, f32[64]{0:T(128)}, u32[]{:S(2)}) copy-start(f32[64]{0:T(128)} %param.9) | copy-start | bytes 772
  266.3 103.3 %all-to-all-start.2 = ((bf16[32,2,16384]{2,1,0:T(2,128)(2,1)}), bf16[32,2,16384]{2,1,0:T(2,128)(2,1)}, u32[]{:S(2)}, u32[]{:S(2)}) async-start(bf16[32,2,16384]{2,1,0:T(2,128)(2,1)} %reshape.51), calls=%async_computation.2 | async-start | bytes 4194304 | tf_op jit(solution)/shard_map/all_to_all | solution.py:53
Sparse Core Ops, SparseCore 0:
  11.6 73.0 all-gather.8
  88.3 78.7 all-gather.10
  170.8 78.7 all-gather.12
where the time goes:
time: 401 us; the launch traced here: 398 us
  waiting for transfers between devices  162 us (40%)
  local copies, waits for them, and re-layouts  112 us (28%)
  blocking collectives  55.7 us (14%)
  other arithmetic  36 us (9%)
  starting transfers between devices  17.9 us (4%)
  between operations  13.9 us (3%)
    all_gather x3, waiting for transfers between devices, total_of_pieces(): return lax.all_gather(value, axis).sum(0)  162 us
    unnamed x13, local copies, waits for them, and re-layouts  67.9 us
    all_gather x5, blocking collectives, gather_in_order(): pieces = lax.all_gather(pieces, axes[k], axis=0, tiled=True)  55.7 us
    unnamed x4, other arithmetic  20.6 us
    all_to_all x2, local copies, waits for them, and re-layouts, on_device(): lax.all_to_all(narrow_gate, SHARD, split_axis=2, concat_axis=1, tiled=True)  13.6 us
    all_to_all x2, local copies, waits for them, and re-layouts, on_device(): lax.all_to_all(narrow_up, SHARD, split_axis=2, concat_axis=1, tiled=True)  13.6 us
    all_to_all x2, local copies, waits for them, and re-layouts, on_device(): lax.all_to_all(narrow_down, SHARD, split_axis=1, concat_axis=2, tiled=True)  13.6 us
  transfers between devices with their start and end apart: 6, of which 3 were waited for; matrix products, arithmetic and copies ran while one was open for 27% of the time, Pallas kernels for 0%

commit v1 on v0

v1 whole, which is shorter than its diff:
```python
import functools

import jax
import jax.numpy as jnp
from jax import lax
from jax.experimental import pallas as pl
from jax.experimental.pallas import tpu as pltpu
from jax.sharding import Mesh
from jax.sharding import PartitionSpec as P

SHARD = ("shard_0", "shard_1", "shard_2")
EXPERT = ("expert_0", "expert_1")
MESH = pl.DeviceIdType.MESH

ORDER = tuple(
    ((k * 11) % 32 // 8, (k * 11) % 8 // 2, (k * 11) % 2) for k in range(1, 32)
)
PAIRS = 8
CUT = 8
CHUNKS = 3 * PAIRS // CUT


def place():
    xl, core, z, y, xh = (lax.axis_index(a) for a in EXPERT + SHARD)
    return xl, core, z, y, xh


def peer(where, offset):
    xl, core, z, y, xh = where
    dz, dy, dx = offset
    turn = 1 - 2 * core
    pz, py, px = (z + turn * dz + 4) % 4, (y + turn * dy + 4) % 4, (xh + dx) % 2
    return (xl, core, pz, py, px), (pz * 4 + py) * 2 + px


def exchange(
    gate, up, down, router, gain,
    landed, routed, scales,
    rows, part, parts, scale, ready, mine,
    load_sem, sum_send, sum_recv, all_send, all_recv,
    data_send, data_recv, own_sem, r_send, r_recv, g_send, g_recv, r_own,
):
    where = place()
    xl, core, z, y, xh = where
    block = z * 4 + y
    me = block * 2 + xh
    group = xl * 2 + core
    peers = [peer(where, offset) for offset in ORDER]
    planes = [(xl, core, (z + dz) % 4, (y + dy) % 4, xh) for dz in range(4) for dy in range(4) if dz or dy]
    twins = ((xl, 1 - core, z, y, xh), (1 - xl, core, z, y, xh))

    loads = [
        pltpu.make_async_copy(source, rows.at[t], load_sem.at[t])
        for t, source in enumerate((gate, up, down))
    ]
    for load in loads:
        load.start()
    barrier = pltpu.get_barrier_semaphore()
    for device, _ in peers:
        pl.semaphore_signal(barrier, inc=1, device_id=device, device_id_type=MESH)
    for device in twins:
        pl.semaphore_signal(barrier, inc=1, device_id=device, device_id_type=MESH)

    narrow = (router[...] * gain[...]).astype(jnp.bfloat16).astype(jnp.float32)
    mine[...] = jnp.concatenate([narrow[0:8], narrow[8:16]], axis=1).astype(jnp.bfloat16)

    for t in range(3):
        loads[t].wait()

        def add_up(e, carry):
            for k in range(8):
                value = rows[t, e, :, pl.ds(k * 128, 128)]
                part[t, e, pl.ds(k, 1), :] = jnp.sum(value * value, axis=0, keepdims=True)
            return carry

        lax.fori_loop(0, 16, add_up, 0)
        if t == 0:
            pl.semaphore_wait(barrier, 33)
        for k, (device, index) in enumerate(peers):
            pltpu.make_async_remote_copy(
                part.at[t, index // 2], parts.at[t, me], sum_send.at[t], sum_recv.at[t],
                device_id=device, device_id_type=MESH,
            ).start()
        parts[t, me] = part[t, block]
        if t == 0:
            for device, _ in peers:
                pltpu.make_async_remote_copy(
                    mine, routed.at[group, me], r_send, r_recv, device_id=device, device_id_type=MESH
                ).start()
            own = pltpu.make_async_copy(mine, routed.at[group, me], r_own)
            own.start()
            own.wait()

    for t in range(3):
        pltpu.make_async_copy(parts.at[t, pl.ds(0, 31)], parts.at[t, pl.ds(0, 31)], sum_recv.at[t]).wait()
        total = parts[t, 0]
        for s in range(1, 32):
            total = total + parts[t, s]
        scale[t, block] = jnp.sqrt(total)
        for device in planes:
            pltpu.make_async_remote_copy(
                scale.at[t, block], scale.at[t, block], all_send.at[t], all_recv.at[t],
                device_id=device, device_id_type=MESH,
            ).start()

    for t in range(3):
        pltpu.make_async_copy(scale.at[t, pl.ds(0, 15)], scale.at[t, pl.ds(0, 15)], all_recv.at[t]).wait()

        def narrowed(p, carry):
            q = t * (PAIRS // CUT) + p // CUT
            for k in range(8):
                low = rows[t, 2 * p, :, pl.ds(k * 128, 128)] * (1.0 / scale[t, 2 * p, pl.ds(k, 1), :])
                high = rows[t, 2 * p + 1, :, pl.ds(k * 128, 128)] * (1.0 / scale[t, 2 * p + 1, pl.ds(k, 1), :])
                both = jnp.concatenate([low, high], axis=0)
                ready[q, pl.ds(4 * k, 4), p % CUT] = both.T.astype(jnp.bfloat16).reshape(4, 32, 128)
            return carry

        for part_of in range(PAIRS // CUT):
            q = t * (PAIRS // CUT) + part_of
            lax.fori_loop(part_of * CUT, part_of * CUT + CUT, narrowed, 0)
            for device, index in peers:
                pltpu.make_async_remote_copy(
                    ready.at[q, index], landed.at[q, me], data_send.at[q], data_recv.at[q],
                    device_id=device, device_id_type=MESH,
                ).start()
            pltpu.make_async_copy(ready.at[q, me], landed.at[q, me], own_sem.at[q]).start()
        rolled = pltpu.roll(scale[t, :, me // 4, :], (128 - 32 * (me % 4)) % 128, 1)
        scales[t] = rolled[:, 0:32]
        if t == 0:
            pltpu.make_async_copy(routed.at[group, pl.ds(0, 31)], routed.at[group, pl.ds(0, 31)], r_recv).wait()
            for k, device in enumerate(twins):
                pltpu.make_async_remote_copy(
                    routed.at[group], routed.at[group], g_send.at[k], g_recv.at[k], device_id=device, device_id_type=MESH
                ).start()
        if t == 1:
            pltpu.make_async_copy(routed.at[0], routed.at[0], g_recv.at[1]).wait()
            other = (1 - xl) * 2 + core
            pltpu.make_async_remote_copy(
                routed.at[other], routed.at[other], g_send.at[2], g_recv.at[2], device_id=twins[0], device_id_type=MESH
            ).start()

    for k in (0, 2):
        pltpu.make_async_copy(routed.at[0], routed.at[0], g_recv.at[k]).wait()
    for k in range(3):
        pltpu.make_async_copy(routed.at[0], routed.at[0], g_send.at[k]).wait()
    pltpu.make_async_copy(routed.at[0, pl.ds(0, 31)], routed.at[0, pl.ds(0, 31)], r_send).wait()
    for t in range(3):
        pltpu.make_async_copy(parts.at[t, pl.ds(0, 31)], parts.at[t, pl.ds(0, 31)], sum_send.at[t]).wait()
        pltpu.make_async_copy(scale.at[t, pl.ds(0, 15)], scale.at[t, pl.ds(0, 15)], all_send.at[t]).wait()
    for q in range(CHUNKS):
        pltpu.make_async_copy(ready.at[q, me], landed.at[q, me], own_sem.at[q]).wait()
        pltpu.make_async_copy(ready.at[q, pl.ds(0, 31)], ready.at[q, pl.ds(0, 31)], data_send.at[q]).wait()
        pltpu.make_async_copy(ready.at[q, pl.ds(0, 31)], ready.at[q, pl.ds(0, 31)], data_recv.at[q]).wait()


def moved(gate, up, down, router, gain):
    hbm = pl.BlockSpec(memory_space=pl.ANY)
    vmem = pl.BlockSpec(memory_space=pltpu.VMEM)
    dma = pltpu.SemaphoreType.DMA
    return pl.pallas_call(
        exchange,
        name="exchange",
        out_shape=(
            jax.ShapeDtypeStruct((CHUNKS, 32, CUT, 32, 128), jnp.bfloat16),
            jax.ShapeDtypeStruct((4, 32, 8, 128), jnp.bfloat16),
            jax.ShapeDtypeStruct((3, 16, 32), jnp.float32),
        ),
        in_specs=[hbm, hbm, hbm, vmem, vmem],
        out_specs=(hbm, hbm, vmem),
        scratch_shapes=[
            pltpu.VMEM((3, 16, 64, 1024), jnp.float32),
            pltpu.VMEM((3, 16, 8, 128), jnp.float32),
            pltpu.VMEM((3, 32, 8, 128), jnp.float32),
            pltpu.VMEM((3, 16, 8, 128), jnp.float32),
            pltpu.VMEM((CHUNKS, 32, CUT, 32, 128), jnp.bfloat16),
            pltpu.VMEM((8, 128), jnp.bfloat16),
            dma((3,)), dma((3,)), dma((3,)), dma((3,)), dma((3,)),
            dma((CHUNKS,)), dma((CHUNKS,)), dma((CHUNKS,)),
            dma, dma, dma((3,)), dma((3,)), dma,
        ],
        compiler_params=pltpu.CompilerParams(collective_id=0, has_side_effects=True),
    )(gate, up, down, router, gain)


STEP = 4


def halves(first, second):
    low = jnp.concatenate([first[..., 0:64], second[..., 0:64]], axis=-1)
    high = jnp.concatenate([first[..., 64:128], second[..., 64:128]], axis=-1)
    return low, high


def settle(landed, routed, gate, up, down, router):
    t, step = pl.program_id(0), pl.program_id(1)

    @pl.when((t == 0) & (step == 0))
    def _():
        for g in range(4):
            for k in range(16):
                low, high = halves(routed[g, 2 * k], routed[g, 2 * k + 1])
                router[pl.ds(16 * g, 8), pl.ds(k * 128, 128)] = low
                router[pl.ds(16 * g + 8, 8), pl.ds(k * 128, 128)] = high

    for at, out in enumerate((gate, up, down)):

        @pl.when(t == at)
        def _():
            def put(p, carry):
                for k in range(16):
                    low, high = halves(landed[0, 2 * k, p], landed[0, 2 * k + 1, p])
                    out[2 * p, :, pl.ds(k * 128, 128)] = low
                    out[2 * p + 1, :, pl.ds(k * 128, 128)] = high
                return carry

            lax.fori_loop(0, STEP, put, 0)


def settled(landed, routed):
    steps, per = PAIRS // STEP, CUT // STEP

    def spot(at):
        return lambda t, s: (jnp.where(t == at, s, jnp.where(t < at, 0, steps - 1)), 0, 0)

    return pl.pallas_call(
        settle,
        name="settle",
        grid=(3, steps),
        out_shape=tuple(jax.ShapeDtypeStruct((16, 32, 2048), jnp.bfloat16) for _ in range(3))
        + (jax.ShapeDtypeStruct((64, 2048), jnp.bfloat16),),
        in_specs=[
            pl.BlockSpec(
                (1, 32, STEP, 32, 128),
                lambda t, s: (t * (PAIRS // CUT) + s // per, 0, s % per, 0, 0),
            ),
            pl.BlockSpec((4, 32, 8, 128), lambda t, s: (0, 0, 0, 0)),
        ],
        out_specs=tuple(pl.BlockSpec((2 * STEP, 32, 2048), spot(at)) for at in range(3))
        + (pl.BlockSpec((64, 2048), lambda t, s: (0, 0)),),
        compiler_params=pltpu.CompilerParams(dimension_semantics=("arbitrary", "arbitrary")),
    )(landed, routed)


def on_device(master_gate, master_up, master_down, router_weight, router_gain):
    landed, routed, scales = moved(
        master_gate, master_up, master_down.transpose(0, 2, 1), router_weight.T, router_gain.reshape(1, 64)
    )
    gate, up, down, router = settled(landed, routed)
    return (
        gate.transpose(0, 2, 1), up.transpose(0, 2, 1), down,
        scales[0], scales[1], scales[2], router.T,
    )


def solution(mesh):
    torus = Mesh(
        mesh.devices.reshape(2, 2, 4, 4, 2),
        ("expert_0", "expert_1", "shard_0", "shard_1", "shard_2"),
    )
    return jax.shard_map(
        on_device,
        mesh=torus,
        in_specs=(
            P(EXPERT, SHARD, None),
            P(EXPERT, SHARD, None),
            P(EXPERT, None, SHARD),
            P(SHARD, EXPERT),
            P(SHARD),
        ),
        out_specs=(
            P(EXPERT, None, SHARD),
            P(EXPERT, None, SHARD),
            P(EXPERT, SHARD, None),
            P(EXPERT, SHARD),
            P(EXPERT, SHARD),
            P(EXPERT, SHARD),
            P(),
        ),
        check_vma=False,
    )
```

time: 401 us -> 108 us (0.27)
  the two profiles are of different devices: /device:TPU:0 before, /device:TPU:14 now
where the time goes in v1:
time: 108 us; the launch traced here: 107 us
  Pallas kernels  106 us (98%)
    pallas_call x1, Pallas kernels, moved(): pl.pallas_call(exchange, name='exchange', out_shape=(jax.ShapeDtypeStruct...  97.3 us
    pallas_call x1, Pallas kernels, settled(): pl.pallas_call(settle, name='settle', grid=(3, steps), out_shape=tuple((j...  8.87 us

profile of v1, /device:TPU:14, one launch (start us, length us, event | category | flops | bytes accessed | tf_op | source)
XLA Modules:
  0.0 107.4 jit_solution(17952962629261204688)
XLA Ops:
  0.6 97.3 %exchange.1 = (bf16[3,32,8,32,128]{4,3,2,1,0:T(8,128)(2,1)}, bf16[4,32,8,128]{3,2,1,0:T(8,128)(2,1)}, f32[3,16,32]{2,1,0:T(8,128)}) custom-call(f32[16,64,1024]{2,1,0:T(8,128)} %gate.1, f32[16,64,1024]{2,1,0:T(8,128)} %up.1, f32[16,64,1024]{2,1,0:T(8,128)} %bitcast.12, f32[16,64]{1,0:T(8,128)} %bitcast.13, f32[1,64]{1,0:T(1,128)} %bitcast.14), custom_call_target="tpu_custom_call" | custom-call | tf_op jit(solution)/shard_map/exchange/pallas_call | solution.py:160
  97.9 0.0 copy-start
  98.0 8.9 %settle.1 = (bf16[16,32,2048]{2,1,0:T(8,128)(2,1)}, bf16[16,32,2048]{2,1,0:T(8,128)(2,1)}, bf16[16,32,2048]{2,1,0:T(8,128)(2,1)}, bf16[64,2048]{1,0:T(8,128)(2,1)}) custom-call(bf16[3,32,8,32,128]{4,3,2,1,0:T(8,128)(2,1)} %get-tuple-element.14.landed, bf16[4,32,8,128]{3,2,1,0:T(8,128)(2,1)} %get-tuple-element.15.routed), custom_call_target="tpu_custom_call" | custom-call | tf_op jit(solution)/shard_map/settle/pallas_call | solution.py:225
  106.8 0.0 copy-done
  106.8 0.6 slice_bitcast_fusion
Async XLA Ops:
  97.9 8.9 %copy-start = (f32[3,16,32]{2,1,0:T(8,128)S(1)}, f32[3,16,32]{2,1,0:T(8,128)}, u32[]{:S(2)}) copy-start(f32[3,16,32]{2,1,0:T(8,128)} %get-tuple-element.19) | copy-start | bytes 18436

commit v2 on v1

--- a/solution.py
+++ b/solution.py
@@ -16,7 +16,7 @@
     ((k * 11) % 32 // 8, (k * 11) % 8 // 2, (k * 11) % 2) for k in range(1, 32)
 )
 PAIRS = 8
-CUT = 8
+CUT = 4
 CHUNKS = 3 * PAIRS // CUT
 
 
@@ -33,10 +33,16 @@
     return (xl, core, pz, py, px), (pz * 4 + py) * 2 + px
 
 
+def halves(first, second):
+    low = jnp.concatenate([first[..., 0:64], second[..., 0:64]], axis=-1)
+    high = jnp.concatenate([first[..., 64:128], second[..., 64:128]], axis=-1)
+    return low, high
+
+
 def exchange(
-    gate, up, down, router, gain,
-    landed, routed, scales,
-    rows, part, parts, scale, ready, mine,
+    gate, up, down, router_at, gain_at,
+    out_gate, out_up, out_down, out_router, scale_gate, scale_up, scale_down,
+    landed, routed, router, gain, rows, part, parts, scale, ready, mine,
     load_sem, sum_send, sum_recv, all_send, all_recv,
     data_send, data_recv, own_sem, r_send, r_recv, g_send, g_recv, r_own,
 ):
@@ -55,12 +61,20 @@
     ]
     for load in loads:
         load.start()
+    smalls = [
+        pltpu.make_async_copy(source, target, load_sem.at[3 + k])
+        for k, (source, target) in enumerate(((router_at, router), (gain_at, gain)))
+    ]
+    for load in smalls:
+        load.start()
     barrier = pltpu.get_barrier_semaphore()
     for device, _ in peers:
         pl.semaphore_signal(barrier, inc=1, device_id=device, device_id_type=MESH)
     for device in twins:
         pl.semaphore_signal(barrier, inc=1, device_id=device, device_id_type=MESH)
 
+    for load in smalls:
+        load.wait()
     narrow = (router[...] * gain[...]).astype(jnp.bfloat16).astype(jnp.float32)
     mine[...] = jnp.concatenate([narrow[0:8], narrow[8:16]], axis=1).astype(jnp.bfloat16)
 
@@ -125,7 +139,7 @@
                 ).start()
             pltpu.make_async_copy(ready.at[q, me], landed.at[q, me], own_sem.at[q]).start()
         rolled = pltpu.roll(scale[t, :, me // 4, :], (128 - 32 * (me % 4)) % 128, 1)
-        scales[t] = rolled[:, 0:32]
+        (scale_gate, scale_up, scale_down)[t][...] = rolled[:, 0:32]
         if t == 0:
             pltpu.make_async_copy(routed.at[group, pl.ds(0, 31)], routed.at[group, pl.ds(0, 31)], r_recv).wait()
             for k, device in enumerate(twins):
@@ -139,8 +153,33 @@
                 routed.at[other], routed.at[other], g_send.at[2], g_recv.at[2], device_id=twins[0], device_id_type=MESH
             ).start()
 
-    for k in (0, 2):
-        pltpu.make_async_copy(routed.at[0], routed.at[0], g_recv.at[k]).wait()
+    for t, out in enumerate((out_gate, out_up, out_down)):
+        for part_of in range(PAIRS // CUT):
+            q = t * (PAIRS // CUT) + part_of
+            pltpu.make_async_copy(ready.at[q, me], landed.at[q, me], own_sem.at[q]).wait()
+            pltpu.make_async_copy(ready.at[q, pl.ds(0, 31)], ready.at[q, pl.ds(0, 31)], data_recv.at[q]).wait()
+
+            def put(p, carry):
+                for k in range(16):
+                    low, high = halves(landed[q, 2 * k, p], landed[q, 2 * k + 1, p])
+                    expert = 2 * (part_of * CUT + p)
+                    out[expert, :, pl.ds(k * 128, 128)] = low
+                    out[expert + 1, :, pl.ds(k * 128, 128)] = high
+                return carry
+
+            lax.fori_loop(0, CUT, put, 0)
+        if t == 1:
+            for k in (0, 2):
+                pltpu.make_async_copy(routed.at[0], routed.at[0], g_recv.at[k]).wait()
+
+            def put_router(g, carry):
+                for k in range(16):
+                    low, high = halves(routed[g, 2 * k], routed[g, 2 * k + 1])
+                    out_router[pl.ds(pl.multiple_of(16 * g, 16), 16), pl.ds(k * 128, 128)] = jnp.concatenate([low, high], axis=0)
+                return carry
+
+            lax.fori_loop(0, 4, put_router, 0)
+
     for k in range(3):
         pltpu.make_async_copy(routed.at[0], routed.at[0], g_send.at[k]).wait()
     pltpu.make_async_copy(routed.at[0, pl.ds(0, 31)], routed.at[0, pl.ds(0, 31)], r_send).wait()
@@ -148,9 +187,7 @@
         pltpu.make_async_copy(parts.at[t, pl.ds(0, 31)], parts.at[t, pl.ds(0, 31)], sum_send.at[t]).wait()
         pltpu.make_async_copy(scale.at[t, pl.ds(0, 15)], scale.at[t, pl.ds(0, 15)], all_send.at[t]).wait()
     for q in range(CHUNKS):
-        pltpu.make_async_copy(ready.at[q, me], landed.at[q, me], own_sem.at[q]).wait()
         pltpu.make_async_copy(ready.at[q, pl.ds(0, 31)], ready.at[q, pl.ds(0, 31)], data_send.at[q]).wait()
-        pltpu.make_async_copy(ready.at[q, pl.ds(0, 31)], ready.at[q, pl.ds(0, 31)], data_recv.at[q]).wait()
 
 
 def moved(gate, up, down, router, gain):
@@ -160,96 +197,58 @@
     return pl.pallas_call(
         exchange,
         name="exchange",
-        out_shape=(
-            jax.ShapeDtypeStruct((CHUNKS, 32, CUT, 32, 128), jnp.bfloat16),
-            jax.ShapeDtypeStruct((4, 32, 8, 128), jnp.bfloat16),
-            jax.ShapeDtypeStruct((3, 16, 32), jnp.float32),
-        ),
-        in_specs=[hbm, hbm, hbm, vmem, vmem],
-        out_specs=(hbm, hbm, vmem),
+        out_shape=tuple(pltpu.VMEM((16, 32, 2048), jnp.bfloat16) for _ in range(3))
+        + (pltpu.VMEM((64, 2048), jnp.bfloat16),)
+        + tuple(pltpu.VMEM((16, 32), jnp.float32) for _ in range(3)),
+        in_specs=[hbm] * 5,
+        out_specs=(vmem,) * 7,
         scratch_shapes=[
+            pltpu.VMEM((CHUNKS, 32, CUT, 32, 128), jnp.bfloat16),
+            pltpu.VMEM((4, 32, 8, 128), jnp.bfloat16),
+            pltpu.VMEM((16, 64), jnp.float32),
+            pltpu.VMEM((1, 64), jnp.float32),
             pltpu.VMEM((3, 16, 64, 1024), jnp.float32),
             pltpu.VMEM((3, 16, 8, 128), jnp.float32),
             pltpu.VMEM((3, 32, 8, 128), jnp.float32),
             pltpu.VMEM((3, 16, 8, 128), jnp.float32),
             pltpu.VMEM((CHUNKS, 32, CUT, 32, 128), jnp.bfloat16),
             pltpu.VMEM((8, 128), jnp.bfloat16),
-            dma((3,)), dma((3,)), dma((3,)), dma((3,)), dma((3,)),
+            dma((5,)), dma((3,)), dma((3,)), dma((3,)), dma((3,)),
             dma((CHUNKS,)), dma((CHUNKS,)), dma((CHUNKS,)),
             dma, dma, dma((3,)), dma((3,)), dma,
         ],
-        compiler_params=pltpu.CompilerParams(collective_id=0, has_side_effects=True),
+        compiler_params=pltpu.CompilerParams(collective_id=0, has_side_effects=True, vmem_limit_bytes=54 * 2**20),
     )(gate, up, down, router, gain)
 
 
-STEP = 4
-
-
-def halves(first, second):
-    low = jnp.concatenate([first[..., 0:64], second[..., 0:64]], axis=-1)
-    high = jnp.concatenate([first[..., 64:128], second[..., 64:128]], axis=-1)
-    return low, high
-
-
-def settle(landed, routed, gate, up, down, router):
-    t, step = pl.program_id(0), pl.program_id(1)
-
-    @pl.when((t == 0) & (step == 0))
-    def _():
-        for g in range(4):
-            for k in range(16):
-                low, high = halves(routed[g, 2 * k], routed[g, 2 * k + 1])
-                router[pl.ds(16 * g, 8), pl.ds(k * 128, 128)] = low
-                router[pl.ds(16 * g + 8, 8), pl.ds(k * 128, 128)] = high
-
-    for at, out in enumerate((gate, up, down)):
-
-        @pl.when(t == at)
-        def _():
-            def put(p, carry):
-                for k in range(16):
-                    low, high = halves(landed[0, 2 * k, p], landed[0, 2 * k + 1, p])
-                    out[2 * p, :, pl.ds(k * 128, 128)] = low
-                    out[2 * p + 1, :, pl.ds(k * 128, 128)] = high
-                return carry
-
-            lax.fori_loop(0, STEP, put, 0)
-
-
-def settled(landed, routed):
-    steps, per = PAIRS // STEP, CUT // STEP
-
-    def spot(at):
-        return lambda t, s: (jnp.where(t == at, s, jnp.where(t < at, 0, steps - 1)), 0, 0)
-
+def write_out(*refs):
+    sources, targets, sem = refs[:7], refs[7:14], refs[14]
+    copies = [pltpu.make_async_copy(sources[k], targets[k], sem.at[k]) for k in range(7)]
+    for copy in copies:
+        copy.start()
+    for copy in copies:
+        copy.wait()
+
+
+def written(arrays):
+    hbm = pl.BlockSpec(memory_space=pltpu.HBM)
+    vmem = pl.BlockSpec(memory_space=pltpu.VMEM)
     return pl.pallas_call(
-        settle,
-        name="settle",
-        grid=(3, steps),
-        out_shape=tuple(jax.ShapeDtypeStruct((16, 32, 2048), jnp.bfloat16) for _ in range(3))
-        + (jax.ShapeDtypeStruct((64, 2048), jnp.bfloat16),),
-        in_specs=[
-            pl.BlockSpec(
-                (1, 32, STEP, 32, 128),
-                lambda t, s: (t * (PAIRS // CUT) + s // per, 0, s % per, 0, 0),
-            ),
-            pl.BlockSpec((4, 32, 8, 128), lambda t, s: (0, 0, 0, 0)),
-        ],
-        out_specs=tuple(pl.BlockSpec((2 * STEP, 32, 2048), spot(at)) for at in range(3))
-        + (pl.BlockSpec((64, 2048), lambda t, s: (0, 0)),),
-        compiler_params=pltpu.CompilerParams(dimension_semantics=("arbitrary", "arbitrary")),
-    )(landed, routed)
+        write_out,
+        name="write_out",
+        out_shape=tuple(jax.ShapeDtypeStruct(v.shape, v.dtype) for v in arrays),
+        in_specs=[vmem] * 7,
+        out_specs=(hbm,) * 7,
+        scratch_shapes=[pltpu.SemaphoreType.DMA((7,))],
+        compiler_params=pltpu.CompilerParams(vmem_limit_bytes=2**20),
+    )(*(pltpu.with_memory_space_constraint(v, pltpu.VMEM) for v in arrays))
 
 
 def on_device(master_gate, master_up, master_down, router_weight, router_gain):
-    landed, routed, scales = moved(
-        master_gate, master_up, master_down.transpose(0, 2, 1), router_weight.T, router_gain.reshape(1, 64)
-    )
-    gate, up, down, router = settled(landed, routed)
-    return (
-        gate.transpose(0, 2, 1), up.transpose(0, 2, 1), down,
-        scales[0], scales[1], scales[2], router.T,
-    )
+    held = (master_gate, master_up, master_down.transpose(0, 2, 1), router_weight.T, router_gain.reshape(1, 64))
+    moved_arrays = moved(*(pltpu.with_memory_space_constraint(v, pltpu.HBM) for v in held))
+    gate, up, down, router, *scales = written(moved_arrays)
+    return (gate.transpose(0, 2, 1), up.transpose(0, 2, 1), down, *scales, router.T)
 
 
 def solution(mesh):

time: 108 us -> 97.9 us (0.906)
  the two profiles are of different devices: /device:TPU:14 before, /device:TPU:0 now
where the time goes in v2:
time: 97.9 us; the launch traced here: 97.8 us
  Pallas kernels  97.2 us (99%)
    pallas_call x1, Pallas kernels, moved(): pl.pallas_call(exchange, name='exchange', out_shape=tuple((pltpu.VMEM((16...  94.4 us
    pallas_call x1, Pallas kernels, written(): pl.pallas_call(write_out, name='write_out', out_shape=tuple((jax.ShapeDty...  2.78 us

profile of v2, /device:TPU:0, one launch (start us, length us, event | category | flops | bytes accessed | tf_op | source)
XLA Modules:
  0.0 97.8 jit_solution(10373267795379816710)
XLA Ops:
  0.6 94.4 %exchange.1 = (bf16[16,32,2048]{2,1,0:T(8,128)(2,1)S(1)}, bf16[16,32,2048]{2,1,0:T(8,128)(2,1)S(1)}, bf16[16,32,2048]{2,1,0:T(8,128)(2,1)S(1)}, bf16[64,2048]{1,...) custom-call(f32[16,64,1024]{2,1,0:T(8,128)} %gate.1, f32[16,64,1024]{2,1,0:T(8,128)} %up.1, ...), custom_call_target="tpu_custom_call" | custom-call | tf_op jit(solution)/shard_map/exchange/pallas_call | solution.py:197
  95.0 2.8 %write_out.1 = (bf16[16,32,2048]{2,1,0:T(8,128)(2,1)}, bf16[16,32,2048]{2,1,0:T(8,128)(2,1)}, bf16[16,32,2048]{2,1,0:T(8,128)(2,1)}, bf16[64,2048]{1,0:T(8,128)(...) custom-call(bf16[16,32,2048]{2,1,0:T(8,128)(2,1)S(1)} %get-tuple-element.21.refs_0_, ...), custom_call_target="tpu_custom_call" | custom-call | tf_op jit(solution)/shard_map/write_out/pallas_call | solution.py:236

commit v3 on v2

--- a/solution.py
+++ b/solution.py
@@ -13,10 +13,12 @@
 MESH = pl.DeviceIdType.MESH
 
 ORDER = tuple(
-    ((k * 11) % 32 // 8, (k * 11) % 8 // 2, (k * 11) % 2) for k in range(1, 32)
+    (a, (a + step) % 4, (a + half) % 2)
+    for step in range(4) for half in range(2) for a in range(4)
+    if (a, (a + step) % 4, (a + half) % 2) != (0, 0, 0)
 )
 PAIRS = 8
-CUT = 4
+CUT = 2
 CHUNKS = 3 * PAIRS // CUT
 
 
@@ -53,14 +55,13 @@
     group = xl * 2 + core
     peers = [peer(where, offset) for offset in ORDER]
     planes = [(xl, core, (z + dz) % 4, (y + dy) % 4, xh) for dz in range(4) for dy in range(4) if dz or dy]
-    twins = ((xl, 1 - core, z, y, xh), (1 - xl, core, z, y, xh))
+    twins = ((xl, 1 - core, z, y, xh), (1 - xl, core, z, y, xh), (1 - xl, core, z, y, 1 - xh))
 
     loads = [
         pltpu.make_async_copy(source, rows.at[t], load_sem.at[t])
         for t, source in enumerate((gate, up, down))
     ]
-    for load in loads:
-        load.start()
+    loads[0].start()
     smalls = [
         pltpu.make_async_copy(source, target, load_sem.at[3 + k])
         for k, (source, target) in enumerate(((router_at, router), (gain_at, gain)))
@@ -80,6 +81,8 @@
 
     for t in range(3):
         loads[t].wait()
+        if t < 2:
+            loads[t + 1].start()
 
         def add_up(e, carry):
             for k in range(8):
@@ -89,7 +92,7 @@
 
         lax.fori_loop(0, 16, add_up, 0)
         if t == 0:
-            pl.semaphore_wait(barrier, 33)
+            pl.semaphore_wait(barrier, 34)
         for k, (device, index) in enumerate(peers):
             pltpu.make_async_remote_copy(
                 part.at[t, index // 2], parts.at[t, me], sum_send.at[t], sum_recv.at[t],
@@ -132,7 +135,8 @@
         for part_of in range(PAIRS // CUT):
             q = t * (PAIRS // CUT) + part_of
             lax.fori_loop(part_of * CUT, part_of * CUT + CUT, narrowed, 0)
-            for device, index in peers:
+            first = q * 5 % 31
+            for device, index in peers[first:] + peers[:first]:
                 pltpu.make_async_remote_copy(
                     ready.at[q, index], landed.at[q, me], data_send.at[q], data_recv.at[q],
                     device_id=device, device_id_type=MESH,
@@ -142,15 +146,20 @@
         (scale_gate, scale_up, scale_down)[t][...] = rolled[:, 0:32]
         if t == 0:
             pltpu.make_async_copy(routed.at[group, pl.ds(0, 31)], routed.at[group, pl.ds(0, 31)], r_recv).wait()
-            for k, device in enumerate(twins):
+            pltpu.make_async_remote_copy(
+                routed.at[group], routed.at[group], g_send.at[0], g_recv.at[0], device_id=twins[0], device_id_type=MESH
+            ).start()
+            for k in range(2):
+                half = routed.at[group, pl.ds(16 * k, 16)]
                 pltpu.make_async_remote_copy(
-                    routed.at[group], routed.at[group], g_send.at[k], g_recv.at[k], device_id=device, device_id_type=MESH
+                    half, half, g_send.at[1 + k], g_recv.at[1 + k], device_id=twins[1 + k], device_id_type=MESH
                 ).start()
         if t == 1:
-            pltpu.make_async_copy(routed.at[0], routed.at[0], g_recv.at[1]).wait()
+            for k in (1, 2):
+                pltpu.make_async_copy(routed.at[0, pl.ds(0, 16)], routed.at[0, pl.ds(0, 16)], g_recv.at[k]).wait()
             other = (1 - xl) * 2 + core
             pltpu.make_async_remote_copy(
-                routed.at[other], routed.at[other], g_send.at[2], g_recv.at[2], device_id=twins[0], device_id_type=MESH
+                routed.at[other], routed.at[other], g_send.at[3], g_recv.at[3], device_id=twins[0], device_id_type=MESH
             ).start()
 
     for t, out in enumerate((out_gate, out_up, out_down)):
@@ -169,7 +178,7 @@
 
             lax.fori_loop(0, CUT, put, 0)
         if t == 1:
-            for k in (0, 2):
+            for k in (0, 3):
                 pltpu.make_async_copy(routed.at[0], routed.at[0], g_recv.at[k]).wait()
 
             def put_router(g, carry):
@@ -180,8 +189,10 @@
 
             lax.fori_loop(0, 4, put_router, 0)
 
-    for k in range(3):
+    for k in (0, 3):
         pltpu.make_async_copy(routed.at[0], routed.at[0], g_send.at[k]).wait()
+    for k in (1, 2):
+        pltpu.make_async_copy(routed.at[0, pl.ds(0, 16)], routed.at[0, pl.ds(0, 16)], g_send.at[k]).wait()
     pltpu.make_async_copy(routed.at[0, pl.ds(0, 31)], routed.at[0, pl.ds(0, 31)], r_send).wait()
     for t in range(3):
         pltpu.make_async_copy(parts.at[t, pl.ds(0, 31)], parts.at[t, pl.ds(0, 31)], sum_send.at[t]).wait()
@@ -215,7 +226,7 @@
             pltpu.VMEM((8, 128), jnp.bfloat16),
             dma((5,)), dma((3,)), dma((3,)), dma((3,)), dma((3,)),
             dma((CHUNKS,)), dma((CHUNKS,)), dma((CHUNKS,)),
-            dma, dma, dma((3,)), dma((3,)), dma,
+            dma, dma, dma((4,)), dma((4,)), dma,
         ],
         compiler_params=pltpu.CompilerParams(collective_id=0, has_side_effects=True, vmem_limit_bytes=54 * 2**20),
     )(gate, up, down, router, gain)

time: 97.9 us -> 95.4 us (0.974)
  Pallas kernels: 97.2 us -> 94.7 us
    pallas_call x1, Pallas kernels: 94.4 us -> 91.9 us  [moved(): pl.pallas_call(exchange, name='exchange', out_shape=tuple((pltpu.VMEM((16...]
where the time goes in v3:
time: 95.4 us; the launch traced here: 95.3 us
  Pallas kernels  94.7 us (99%)
    pallas_call x1, Pallas kernels, moved(): pl.pallas_call(exchange, name='exchange', out_shape=tuple((pltpu.VMEM((16...  91.9 us
    pallas_call x1, Pallas kernels, written(): pl.pallas_call(write_out, name='write_out', out_shape=tuple((jax.ShapeDty...  2.78 us

profile of v3, /device:TPU:0, one launch (start us, length us, event | category | flops | bytes accessed | tf_op | source)
XLA Modules:
  0.0 95.3 jit_solution(17553731613358318906)
XLA Ops:
  0.6 91.9 %exchange.1 = (bf16[16,32,2048]{2,1,0:T(8,128)(2,1)S(1)}, bf16[16,32,2048]{2,1,0:T(8,128)(2,1)S(1)}, bf16[16,32,2048]{2,1,0:T(8,128)(2,1)S(1)}, bf16[64,2048]{1,...) custom-call(f32[16,64,1024]{2,1,0:T(8,128)} %gate.1, f32[16,64,1024]{2,1,0:T(8,128)} %up.1, ...), custom_call_target="tpu_custom_call" | custom-call | tf_op jit(solution)/shard_map/exchange/pallas_call | solution.py:208
  92.5 2.8 %write_out.1 = (bf16[16,32,2048]{2,1,0:T(8,128)(2,1)}, bf16[16,32,2048]{2,1,0:T(8,128)(2,1)}, bf16[16,32,2048]{2,1,0:T(8,128)(2,1)}, bf16[64,2048]{1,0:T(8,128)(...) custom-call(bf16[16,32,2048]{2,1,0:T(8,128)(2,1)S(1)} %get-tuple-element.21.refs_0_, ...), custom_call_target="tpu_custom_call" | custom-call | tf_op jit(solution)/shard_map/write_out/pallas_call | solution.py:247

commit v4 on v3

--- a/solution.py
+++ b/solution.py
@@ -17,8 +17,10 @@
     for step in range(4) for half in range(2) for a in range(4)
     if (a, (a + step) % 4, (a + half) % 2) != (0, 0, 0)
 )
+FAR_FIRST = sorted(range(31), key=lambda k: -sum((0, 1, 2, 1)[v] for v in ORDER[k][:2]) - 2 * ORDER[k][2])
 PAIRS = 8
 CUT = 2
+LAST = 4
 CHUNKS = 3 * PAIRS // CUT
 
 
@@ -120,6 +122,19 @@
                 device_id=device, device_id_type=MESH,
             ).start()
 
+    def turned_by(q):
+        return [(q * 5 + k) % 31 for k in range(31)]
+
+    def send_out(messages):
+        for q, k in messages:
+            device, index = peers[k]
+            pltpu.make_async_remote_copy(
+                ready.at[q, index], landed.at[q, me], data_send.at[q], data_recv.at[q],
+                device_id=device, device_id_type=MESH,
+            ).start()
+        for q in sorted({q for q, _ in messages}):
+            pltpu.make_async_copy(ready.at[q, me], landed.at[q, me], own_sem.at[q]).start()
+
     for t in range(3):
         pltpu.make_async_copy(scale.at[t, pl.ds(0, 15)], scale.at[t, pl.ds(0, 15)], all_recv.at[t]).wait()
 
@@ -135,13 +150,10 @@
         for part_of in range(PAIRS // CUT):
             q = t * (PAIRS // CUT) + part_of
             lax.fori_loop(part_of * CUT, part_of * CUT + CUT, narrowed, 0)
-            first = q * 5 % 31
-            for device, index in peers[first:] + peers[:first]:
-                pltpu.make_async_remote_copy(
-                    ready.at[q, index], landed.at[q, me], data_send.at[q], data_recv.at[q],
-                    device_id=device, device_id_type=MESH,
-                ).start()
-            pltpu.make_async_copy(ready.at[q, me], landed.at[q, me], own_sem.at[q]).start()
+            if q < CHUNKS - LAST:
+                send_out([(q, k) for k in turned_by(q)])
+            elif q == CHUNKS - 1:
+                send_out([(r, k) for k in FAR_FIRST for r in range(CHUNKS - LAST, CHUNKS)])
         rolled = pltpu.roll(scale[t, :, me // 4, :], (128 - 32 * (me % 4)) % 128, 1)
         (scale_gate, scale_up, scale_down)[t][...] = rolled[:, 0:32]
         if t == 0:

time: 95.4 us -> 94.1 us (0.986)
  Pallas kernels: 94.7 us -> 93.4 us
    pallas_call x1, Pallas kernels: 91.9 us -> 90.6 us  [moved(): pl.pallas_call(exchange, name='exchange', out_shape=tuple((pltpu.VMEM((16...]
where the time goes in v4:
time: 94.1 us; the launch traced here: 94 us
  Pallas kernels  93.4 us (99%)
    pallas_call x1, Pallas kernels, moved(): pl.pallas_call(exchange, name='exchange', out_shape=tuple((pltpu.VMEM((16...  90.6 us
    pallas_call x1, Pallas kernels, written(): pl.pallas_call(write_out, name='write_out', out_shape=tuple((jax.ShapeDty...  2.78 us

profile of v4, /device:TPU:0, one launch (start us, length us, event | category | flops | bytes accessed | tf_op | source)
XLA Modules:
  0.0 94.0 jit_solution(4365888497214529390)
XLA Ops:
  0.6 90.6 %exchange.1 = (bf16[16,32,2048]{2,1,0:T(8,128)(2,1)S(1)}, bf16[16,32,2048]{2,1,0:T(8,128)(2,1)S(1)}, bf16[16,32,2048]{2,1,0:T(8,128)(2,1)S(1)}, bf16[64,2048]{1,...) custom-call(f32[16,64,1024]{2,1,0:T(8,128)} %gate.1, f32[16,64,1024]{2,1,0:T(8,128)} %up.1, ...), custom_call_target="tpu_custom_call" | custom-call | tf_op jit(solution)/shard_map/exchange/pallas_call | solution.py:220
  91.2 2.8 %write_out.1 = (bf16[16,32,2048]{2,1,0:T(8,128)(2,1)}, bf16[16,32,2048]{2,1,0:T(8,128)(2,1)}, bf16[16,32,2048]{2,1,0:T(8,128)(2,1)}, bf16[64,2048]{1,0:T(8,128)(...) custom-call(bf16[16,32,2048]{2,1,0:T(8,128)(2,1)S(1)} %get-tuple-element.21.refs_0_, ...), custom_call_target="tpu_custom_call" | custom-call | tf_op jit(solution)/shard_map/write_out/pallas_call | solution.py:259

commit v5 on v4

--- a/solution.py
+++ b/solution.py
@@ -19,8 +19,8 @@
 )
 FAR_FIRST = sorted(range(31), key=lambda k: -sum((0, 1, 2, 1)[v] for v in ORDER[k][:2]) - 2 * ORDER[k][2])
 PAIRS = 8
-CUT = 2
-LAST = 4
+CUT = 4
+LAST = 2
 CHUNKS = 3 * PAIRS // CUT
 
 

time: 94.1 us -> 94.4 us (level)
  no operation moved by 1% of the time
where the time goes in v5:
time: 94.4 us; the launch traced here: 94.3 us
  Pallas kernels  93.7 us (99%)
    pallas_call x1, Pallas kernels, moved(): pl.pallas_call(exchange, name='exchange', out_shape=tuple((pltpu.VMEM((16...  90.9 us
    pallas_call x1, Pallas kernels, written(): pl.pallas_call(write_out, name='write_out', out_shape=tuple((jax.ShapeDty...  2.78 us

profile of v5, /device:TPU:0, one launch (start us, length us, event | category | flops | bytes accessed | tf_op | source)
XLA Modules:
  0.0 94.3 jit_solution(16413821533245436315)
XLA Ops:
  0.6 90.9 %exchange.1 = (bf16[16,32,2048]{2,1,0:T(8,128)(2,1)S(1)}, bf16[16,32,2048]{2,1,0:T(8,128)(2,1)S(1)}, bf16[16,32,2048]{2,1,0:T(8,128)(2,1)S(1)}, bf16[64,2048]{1,...) custom-call(f32[16,64,1024]{2,1,0:T(8,128)} %gate.1, f32[16,64,1024]{2,1,0:T(8,128)} %up.1, ...), custom_call_target="tpu_custom_call" | custom-call | tf_op jit(solution)/shard_map/exchange/pallas_call | solution.py:220
  91.5 2.8 %write_out.1 = (bf16[16,32,2048]{2,1,0:T(8,128)(2,1)}, bf16[16,32,2048]{2,1,0:T(8,128)(2,1)}, bf16[16,32,2048]{2,1,0:T(8,128)(2,1)}, bf16[64,2048]{1,0:T(8,128)(...) custom-call(bf16[16,32,2048]{2,1,0:T(8,128)(2,1)S(1)} %get-tuple-element.21.refs_0_, ...), custom_call_target="tpu_custom_call" | custom-call | tf_op jit(solution)/shard_map/write_out/pallas_call | solution.py:259
